TPU v7x, 32 devices: a whole 2x2x4 slice. The times are simulated.
32 devices in a mesh: grp: 2 (over core), tp: 4 (over y, x), src: 4 (over z).
Axes of the slice: x: 2, y: 2, z: 4, core: 2. Of those that a mesh axis runs over, the one named last changes fastest.
Arguments:
- hidden_in: bfloat16 [512, 5120], P(('grp', 'src')), may hold values from -6 to 6
- attn_gain: float32 [5120], replicated, may hold values from 0.5 to 1.5
- w_qkv: int32 [1280, 5120], P(None, 'tp'), may hold values from -2147483648 to 2147483646
- qkv_scale: float32 [5120], P('tp'), may hold values from 0.0001118034 to 0.00041926274
- q_gain: float32 [128], replicated, may hold values from 0.25 to 1.75
- k_gain: float32 [128], replicated, may hold values from 0.1 to 1.9
- key_cache: bfloat16 [8, 64, 128, 512], P(('grp', 'src'), 'tp'), may hold values from -400 to 400
- value_cache: bfloat16 [8, 64, 128, 512], P(('grp', 'src'), 'tp'), may hold values from -9 to 9
- lengths: int32 [8, 64], P(('grp', 'src'), 'tp'), may hold values from 1 to 128, as said below
- w_out: int32 [1024, 5120], P('tp'), may hold values from -2147483648 to 2147483646
- out_scale: float32 [5120], replicated, may hold values from 0.0003125 to 0.00125
- mlp_gain: float32 [5120], replicated, may hold values from 0.5 to 1.5
- w_gate: int32 [1280, 12800], P(('grp', 'src'), 'tp'), may hold values from -2147483648 to 2147483646
- w_up: int32 [1280, 12800], P(('grp', 'src'), 'tp'), may hold values from -2147483648 to 2147483646
- gate_scale: float32 [12800], P('tp'), may hold values from 0.0001118034 to 0.00041926274
- up_scale: float32 [12800], P('tp'), may hold values from 0.0001118034 to 0.00041926274
- w_down: int32 [3200, 5120], P('tp', ('grp', 'src')), may hold values from -2147483648 to 2147483646
- down_scale: float32 [5120], replicated, may hold values from 0.00013258251 to 0.00053033006
Outputs:
- layer_out: bfloat16 [512, 5120], P(('grp', 'src'), 'tp')
Inputs may be any that keep to these rules, and one draw needn't show every extreme that they name: `lengths`: some sequence has exactly 128 cached positions.
All inputs are finite; a program needn't handle non-finite values.
Results may differ from a plain program's by a relative error of at most 0.028.
Values may be sent and summed in bfloat16 or wider, within the bound.
A program may use at most 128 MiB of HBM per device.

v0:
```python
import math

import jax
import jax.numpy as jnp
from jax import lax
from jax.sharding import PartitionSpec as P

D = 5120
QUERY_HEADS = 32
KEY_VALUE_HEADS = 4
HEAD_SIZE = 128
QUERY_COLUMNS = 4096
KEY_COLUMNS = 512


norm_epsilon = 1e-06
rope_base = 1000000.0


def unpack_bytes(packed, byte_index):
    return jnp.right_shift(jnp.left_shift(packed, 24 - 8 * byte_index), 24)


def byte_product(activations, packed):
    products = [
        jnp.dot(
            activations[:, byte_index::4],
            unpack_bytes(packed, byte_index).astype(jnp.bfloat16),
            preferred_element_type=jnp.float32,
        )
        for byte_index in range(4)
    ]
    return products[0] + products[1] + products[2] + products[3]


def normalize_rows(values, gain_row):
    return (
        values
        * lax.rsqrt(jnp.mean(values * values, axis=-1, keepdims=True) + norm_epsilon)
        * gain_row
    )


def rotary_embed(values, positions):
    half_dim = values.shape[-1] // 2
    freq_index = jnp.arange(half_dim, dtype=jnp.float32)
    inverse = jnp.exp(freq_index * (-math.log(rope_base) / half_dim))
    angles = positions.astype(jnp.float32)[:, None] * inverse[None, :]
    cosine = jnp.cos(angles)[:, None, :]
    sine_part = jnp.sin(angles)[:, None, :]
    lower_half = values[..., :half_dim]
    upper_half = values[..., half_dim:]
    return jnp.concatenate(
        [
            lower_half * cosine - upper_half * sine_part,
            upper_half * cosine + lower_half * sine_part,
        ],
        axis=-1,
    )


def local_attention(query_key_value_rows, q_gain, k_gain, stored_keys, stored_values, seq_lengths):
    count_of_rows = query_key_value_rows.shape[0]
    cache_length = stored_keys.shape[1]
    query_matrix = (
        query_key_value_rows[:, :QUERY_COLUMNS]
        .astype(jnp.float32)
        .reshape(count_of_rows, QUERY_HEADS, HEAD_SIZE)
    )
    incoming_keys = (
        query_key_value_rows[:, QUERY_COLUMNS : QUERY_COLUMNS + KEY_COLUMNS]
        .astype(jnp.float32)
        .reshape(count_of_rows, KEY_VALUE_HEADS, HEAD_SIZE)
    )
    incoming_values = query_key_value_rows[:, QUERY_COLUMNS + KEY_COLUMNS :].reshape(
        count_of_rows, KEY_VALUE_HEADS, HEAD_SIZE
    )
    query_matrix = rotary_embed(normalize_rows(query_matrix, q_gain), seq_lengths).astype(
        jnp.bfloat16
    )
    incoming_keys = rotary_embed(normalize_rows(incoming_keys, k_gain), seq_lengths).astype(
        jnp.bfloat16
    )
    query_groups = query_matrix.reshape(
        count_of_rows, KEY_VALUE_HEADS, QUERY_HEADS // KEY_VALUE_HEADS, HEAD_SIZE
    )
    key_slices = stored_keys.reshape(count_of_rows, cache_length, KEY_VALUE_HEADS, HEAD_SIZE)
    value_slices = stored_values.reshape(count_of_rows, cache_length, KEY_VALUE_HEADS, HEAD_SIZE)
    logit_scale = 1.0 / math.sqrt(HEAD_SIZE)
    scores = (
        jnp.einsum("bkgd,bpkd->bkgp", query_groups, key_slices, preferred_element_type=jnp.float32)
        * logit_scale
    )
    live_mask = jnp.arange(cache_length, dtype=jnp.int32)[None, :] < seq_lengths[:, None]
    scores = jnp.where(live_mask[:, None, None, :], scores, -jnp.inf)
    self_score = (
        jnp.einsum("nufi,nui->nuf", query_groups, incoming_keys, preferred_element_type=jnp.float32)
        * logit_scale
    )
    row_max = jnp.maximum(jnp.max(scores, axis=-1), self_score)
    soft_weights = jnp.exp(scores - row_max[..., None])
    own_weight = jnp.exp(self_score - row_max)
    denominator = jnp.sum(soft_weights, axis=-1) + own_weight
    own_low = lax.optimization_barrier(own_weight.astype(jnp.bfloat16)).astype(jnp.float32)
    numerator = jnp.einsum(
        "bkgp,bpkd->bkgd",
        soft_weights.astype(jnp.bfloat16),
        value_slices,
        preferred_element_type=jnp.float32,
    )
    numerator = numerator + own_low[..., None] * incoming_values.astype(jnp.float32)[:, :, None, :]
    return (
        (numerator / denominator[..., None])
        .reshape(count_of_rows, QUERY_COLUMNS)
        .astype(jnp.bfloat16)
    )


def local(
    hidden_in,
    attn_gain,
    w_qkv,
    qkv_scale,
    q_gain,
    k_gain,
    key_cache,
    value_cache,
    lengths,
    w_out,
    out_scale,
    mlp_gain,
    w_gate,
    w_up,
    gate_scale,
    up_scale,
    w_down,
    down_scale,
):
    tp_count = lax.axis_size("tp")
    tp_index = lax.axis_index("tp")
    share_cols = D // tp_count
    residual = hidden_in.astype(jnp.float32)
    normed = normalize_rows(residual, attn_gain).astype(jnp.bfloat16)
    qkv_part = (byte_product(normed, w_qkv) * qkv_scale).astype(jnp.bfloat16)
    query_key_value_rows = lax.all_to_all(qkv_part, "tp", split_axis=0, concat_axis=1, tiled=True)
    heads_out = local_attention(
        query_key_value_rows, q_gain, k_gain, key_cache[0], value_cache[0], lengths[0]
    )
    head_rows = lax.all_to_all(heads_out, "tp", split_axis=1, concat_axis=0, tiled=True)
    partial_value = byte_product(head_rows, w_out) * out_scale
    attn_full = lax.psum(partial_value.astype(jnp.bfloat16), "tp").astype(jnp.float32)
    mid_full = (residual + attn_full).astype(jnp.bfloat16)
    normed_mlp = normalize_rows(mid_full.astype(jnp.float32), mlp_gain).astype(jnp.bfloat16)
    mid_share = lax.dynamic_slice_in_dim(mid_full, tp_index * share_cols, share_cols, 1)
    gate_total = byte_product(
        normed_mlp, lax.all_gather(w_gate, ("grp", "src"), axis=0, tiled=True)
    )
    up_total = byte_product(normed_mlp, lax.all_gather(w_up, ("grp", "src"), axis=0, tiled=True))
    activated = (jax.nn.silu(gate_total * gate_scale) * (up_total * up_scale)).astype(jnp.bfloat16)
    down_terms = (
        byte_product(activated, lax.all_gather(w_down, ("grp", "src"), axis=1, tiled=True))
        * down_scale
    )
    mlp_share = lax.psum_scatter(
        down_terms.astype(jnp.bfloat16), "tp", scatter_dimension=1, tiled=True
    ).astype(jnp.float32)
    return (mid_share.astype(jnp.float32) + mlp_share).astype(jnp.bfloat16)


def solution(mesh):
    return jax.shard_map(
        local,
        mesh=mesh,
        in_specs=(
            P(("grp", "src"), None),
            P(),
            P(None, "tp"),
            P("tp"),
            P(),
            P(),
            P(("grp", "src"), "tp", None, None),
            P(("grp", "src"), "tp", None, None),
            P(("grp", "src"), "tp"),
            P("tp", None),
            P(),
            P(),
            P(("grp", "src"), "tp"),
            P(("grp", "src"), "tp"),
            P("tp"),
            P("tp"),
            P("tp", ("grp", "src")),
            P(),
        ),
        out_specs=P(("grp", "src"), "tp"),
        check_vma=False,
    )
```

profile of v0, /device:TPU:0, one launch (start us, length us, event | category | flops | bytes accessed | tf_op | source)
XLA Modules:
  0.0 582.0 jit_solution(6829318386932394782)
XLA Ops:
  10.0 6.5 %slice.73 = bf16[64,1280]{1,0:T(8,128)(2,1)S(1)} slice(bf16[64,5120]{1,0:T(8,128)(2,1)S(1)} %fusion.83), slice={[0:64:1], [0:5120:4]} | slice | bytes 327680 | tf_op jit(solution)/shard_map/slice | solution.py:27
  16.6 6.6 %slice.74 = bf16[64,1280]{1,0:T(8,128)(2,1)S(1)} slice(bf16[64,5120]{1,0:T(8,128)(2,1)S(1)} %fusion.83), slice={[0:64:1], [1:5120:4]} | slice | bytes 327680 | tf_op jit(solution)/shard_map/slice | solution.py:27
  23.1 6.5 %slice.75 = bf16[64,1280]{1,0:T(8,128)(2,1)S(1)} slice(bf16[64,5120]{1,0:T(8,128)(2,1)S(1)} %fusion.83), slice={[0:64:1], [2:5120:4]} | slice | bytes 327680 | tf_op jit(solution)/shard_map/slice | solution.py:27
  29.6 6.7 %slice.76 = bf16[64,1280]{1,0:T(8,128)(2,1)S(1)} slice(bf16[64,5120]{1,0:T(8,128)(2,1)S(1)} %fusion.83), slice={[0:64:1], [3:5120:4]} | slice | bytes 327680 | tf_op jit(solution)/shard_map/slice | solution.py:27
  36.4 4.0 fusion.50
  44.8 5.3 all-to-all-start
  50.1 2.6 reshape_squeeze.6
  52.7 4.0 reshape_squeeze.7
  62.3 9.2 %all_to_all.35 = bf16[16,4,1024]{2,0,1:T(8,128)(2,1)S(1)} all-to-all(bf16[16,4,1024]{2,0,1:T(8,128)(2,1)S(1)} %copy.28), channel_id=1, replica_groups=mesh['grp'=2,'tp'=4,'src'=4] {'tp'}, dimensions={1} | all-to-all | bytes 262144 | tf_op jit(solution)/shard_map/all_to_all | solution.py:149
  76.1 3.5 fusion.61
  79.6 3.5 convolution_add_fusion.2
  87.5 44.9 %all-reduce.2.cloned.1.call-done = bf16[64,5120]{1,0:T(8,128)(2,1)} async-done(((bf16[64,5120]{1,0:T(8,128)(2,1)}), bf16[64,5120]{1,0:T(8,128)(2,1)}) %all-reduce.2.cloned.1.call-update) | async-done | bytes 655376 | tf_op jit(solution)/shard_map/psum | solution.py:151
  134.0 7.0 %slice.88 = bf16[64,1280]{1,0:T(8,128)(2,1)S(1)} slice(bf16[64,5120]{1,0:T(8,128)(2,1)S(1)} %fusion.80), slice={[0:64:1], [0:5120:4]} | slice | bytes 327680 | tf_op jit(solution)/shard_map/slice | solution.py:27
  141.0 6.6 %slice.89 = bf16[64,1280]{1,0:T(8,128)(2,1)S(1)} slice(bf16[64,5120]{1,0:T(8,128)(2,1)S(1)} %fusion.80), slice={[0:64:1], [1:5120:4]} | slice | bytes 327680 | tf_op jit(solution)/shard_map/slice | solution.py:27
  147.6 6.5 %slice.90 = bf16[64,1280]{1,0:T(8,128)(2,1)S(1)} slice(bf16[64,5120]{1,0:T(8,128)(2,1)S(1)} %fusion.80), slice={[0:64:1], [2:5120:4]} | slice | bytes 327680 | tf_op jit(solution)/shard_map/slice | solution.py:27
  154.1 6.7 %slice.91 = bf16[64,1280]{1,0:T(8,128)(2,1)S(1)} slice(bf16[64,5120]{1,0:T(8,128)(2,1)S(1)} %fusion.80), slice={[0:64:1], [3:5120:4]} | slice | bytes 327680 | tf_op jit(solution)/shard_map/slice | solution.py:27
  160.8 74.5 %all-gather.4.cloned.1.call-done = s32[1280,3200]{1,0:T(8,128)} async-done(((s32[160,3200]{1,0:T(8,128)}), s32[1280,3200]{1,0:T(8,128)}) %all-gather.4.cloned.1.call-update) | async-done | bytes 16384016 | tf_op jit(solution)/shard_map/all_gather | solution.py:156
  235.3 8.0 %fusion = f32[64,3200]{1,0:T(8,128)S(1)} fusion(bf16[64,1280]{1,0:T(8,128)(2,1)S(1)} %slice.88, s32[1280,3200]{1,0:T(8,128)} %all-gather.4.cloned.1.call-done), kind=kOutput, calls=%fused_computation.12 | convolution fusion | flops 536576000 | bytes 17367040 | tf_op jit(solution)/shard_map/dot_general | solution.py:26
  243.3 139.4 %all-gather.6.cloned.1.call-done = s32[1280,3200]{1,0:T(8,128)} async-done(((s32[160,3200]{1,0:T(8,128)}), s32[1280,3200]{1,0:T(8,128)}) %all-gather.6.cloned.1.call-update) | async-done | bytes 16384016 | tf_op jit(solution)/shard_map/all_gather | solution.py:158
  382.7 8.1 %fusion.4 = f32[64,3200]{1,0:T(8,128)S(1)} fusion(bf16[64,1280]{1,0:T(8,128)(2,1)S(1)} %slice.88, s32[1280,3200]{1,0:T(8,128)} %all-gather.6.cloned.1.call-done), kind=kOutput, calls=%fused_computation.16 | convolution fusion | flops 536576000 | bytes 17367040 | tf_op jit(solution)/shard_map/dot_general | solution.py:26
  390.8 9.9 %fusion.45 = f32[64,3200]{1,0:T(8,128)S(1)} fusion(f32[64,3200]{1,0:T(8,128)S(1)} %fusion, bf16[64,1280]{1,0:T(8,128)(2,1)S(1)} %slice.89, s32[1280,3200]{1,0:T(8,128)} %all-gather.4.cloned.1.call-done), kind=kOutput, calls=%fused_computation.68 | convolution fusion | flops 536780800 | bytes 18186240 | tf_op jit(solution)/shard_map/dot_general | solution.py:26
  403.2 8.0 %fusion.44 = f32[64,3200]{1,0:T(8,128)S(1)} fusion(f32[64,3200]{1,0:T(8,128)S(1)} %fusion.45, bf16[64,1280]{1,0:T(8,128)(2,1)S(1)} %slice.90, s32[1280,3200]{1,0:T(8,128)} %all-gather.4.cloned.1.call-done), kind=kOutput, calls=%fused_computation.67 | convolution fusion | flops 536780800 | bytes 18186240 | tf_op jit(solution)/shard_map/dot_general | solution.py:26
  411.2 2.6 fusion.41
  413.9 7.6 %fusion.46 = f32[64,3200]{1,0:T(8,128)S(1)} fusion(f32[64,3200]{1,0:T(8,128)S(1)} %fusion.44, bf16[64,1280]{1,0:T(8,128)(2,1)S(1)} %slice.91, s32[1280,3200]{1,0:T(8,128)} %all-gather.4.cloned.1.call-done, f32[3200]{0:T(1024)S(1)} %copy-done.7), kind=kOutput, calls=%fused_computation.69 | convolution fusion | flops 536985600 | bytes 18199040 | tf_op jit(solution)/shard_map/dot_general | solution.py:26
  423.5 3.7 slice.92
  427.2 3.7 slice.93
  430.9 3.7 slice.94
  434.6 4.0 slice.95
  438.6 91.5 %all-gather.8.cloned.1.call-done = s32[800,5120]{1,0:T(8,128)} async-done(((s32[800,640]{1,0:T(8,128)}), s32[800,5120]{1,0:T(8,128)}) %all-gather.8.cloned.1.call-update) | async-done | bytes 16384016 | tf_op jit(solution)/shard_map/all_gather | solution.py:161
  530.1 8.2 %fusion.8 = f32[64,5120]{1,0:T(8,128)S(1)} fusion(bf16[64,800]{1,0:T(8,128)(2,1)S(1)} %slice.92, s32[800,5120]{1,0:T(8,128)} %all-gather.8.cloned.1.call-done), kind=kOutput, calls=%fused_computation.20 | convolution fusion | flops 536576000 | bytes 17797120 | tf_op jit(solution)/shard_map/dot_general | solution.py:26
  545.4 2.9 fusion.38
  548.3 24.0 %reduce-scatter.2.cloned.1.call-done = bf16[64,1280]{1,0:T(8,128)(2,1)} async-done(((bf16[64,5120]{1,0:T(8,128)(2,1)}), bf16[64,1280]{1,0:T(8,128)(2,1)}) %reduce-scatter.2.cloned.1.call-update) | async-done | bytes 163856 | tf_op jit(solution)/shard_map/reduce_scatter | solution.py:164
  (97 shorter events, 36.1 us)
Async XLA Ops:
  36.4 4.7 copy-start.1
  41.1 2.1 copy-start.8
  42.2 8.0 %copy-start.11 = (s32[1,16]{1,0:T(1,128)S(1)}, s32[1,16]{1,0:T(1,128)}, u32[]{:S(2)}) copy-start(s32[1,16]{1,0:T(1,128)} %param.26) | copy-start | bytes 196
  44.8 12.5 %copy-start.9 = (f32[128]{0:T(128)S(1)}, f32[128]{0:T(128)}, u32[]{:S(2)}) copy-start(f32[128]{0:T(128)} %param.23) | copy-start | bytes 1540
  44.8 12.6 %copy-start.10 = (f32[128]{0:T(128)S(1)}, f32[128]{0:T(128)}, u32[]{:S(2)}) copy-start(f32[128]{0:T(128)} %param.22) | copy-start | bytes 1540
  44.8 12.1 %all-to-all-start = ((bf16[4,16,1280]{2,1,0:T(8,128)(2,1)}), bf16[4,16,1280]{2,1,0:T(8,128)(2,1)S(1)}, u32[]{:S(2)}, u32[]{:S(2)}) async-start(bf16[4,16,1280]{2,1,0:T(8,128)(2,1)} %bitcast.1), calls=%async_computation | async-start | bytes 327680 | tf_op jit(solution)/shard_map/all_to_all | solution.py:145
  50.1 82.3 %all-reduce.2.cloned.1.call-start = ((), (), s32[]{:S(2)}) async-start(), calls=%async_computation.3 | async-start | bytes 1310720 | tf_op jit(solution)/shard_map/psum | solution.py:151
  76.1 7.0 %slice-start.4 = ((s8[5242880]{0:T(1024)(128)(4,1)}), s8[4194304]{0:T(1024)(128)(4,1)S(1)}, s32[]{:S(2)}) async-start(s8[5242880]{0:T(1024)(128)(4,1)} %bitcast.49), calls=%async_computation.12 | async-start | bytes 8388608
  79.6 3.5 slice-start.5
  79.6 4.4 copy-start.4
  84.0 48.3 %copy-start.2 = (bf16[64,5120]{1,0:T(8,128)(2,1)S(1)}, bf16[64,5120]{1,0:T(8,128)(2,1)}, u32[]{:S(2)}) copy-start(bf16[64,5120]{1,0:T(8,128)(2,1)} %param.18) | copy-start | bytes 1966084
  84.0 49.8 %copy-start.5 = (f32[5120]{0:T(1024)S(1)}, f32[5120]{0:T(1024)}, u32[]{:S(2)}) copy-start(f32[5120]{0:T(1024)} %param.29) | copy-start | bytes 61444
  85.7 149.6 %all-gather.4.cloned.1.call-start = ((), (), s32[]{:S(2)}) async-start(), calls=%async_computation.4 | async-start | bytes 18432000 | tf_op jit(solution)/shard_map/all_gather | solution.py:156
  86.3 296.4 %all-gather.6.cloned.1.call-start = ((), (), s32[]{:S(2)}) async-start(), calls=%async_computation.5 | async-start | bytes 18432000 | tf_op jit(solution)/shard_map/all_gather | solution.py:158
  86.9 443.2 %all-gather.8.cloned.1.call-start = ((), (), s32[]{:S(2)}) async-start(), calls=%async_computation.6 | async-start | bytes 18432000 | tf_op jit(solution)/shard_map/all_gather | solution.py:161
  87.4 484.9 %reduce-scatter.2.cloned.1.call-start = ((), (), s32[]{:S(2)}) async-start(), calls=%async_computation.7 | async-start | bytes 819200 | tf_op jit(solution)/shard_map/reduce_scatter | solution.py:164
  382.7 18.1 %slice-start = ((s8[16384000]{0:T(1024)(128)(4,1)}), s8[4194304]{0:T(1024)(128)(4,1)S(1)}, s32[]{:S(2)}) async-start(s8[16384000]{0:T(1024)(128)(4,1)} %bitcast.47), calls=%async_computation.8 | async-start | bytes 8388608
  382.7 18.1 %slice-start.1 = ((s8[16384000]{0:T(1024)(128)(4,1)}), s8[4194304]{0:T(1024)(128)(4,1)S(1)}, s32[]{:S(2)}) async-start(s8[16384000]{0:T(1024)(128)(4,1)} %bitcast.47), calls=%async_computation.9 | async-start | bytes 8388608
  390.8 9.9 %slice-start.2 = ((s8[16384000]{0:T(1024)(128)(4,1)}), s8[4194304]{0:T(1024)(128)(4,1)S(1)}, s32[]{:S(2)}) async-start(s8[16384000]{0:T(1024)(128)(4,1)} %bitcast.47), calls=%async_computation.10 | async-start | bytes 8388608
  390.8 9.9 %slice-start.3 = ((s8[16384000]{0:T(1024)(128)(4,1)}), s8[3801088]{0:T(1024)(128)(4,1)S(1)}, s32[]{:S(2)}) async-start(s8[16384000]{0:T(1024)(128)(4,1)} %bitcast.47), calls=%async_computation.11 | async-start | bytes 7602176
  411.2 2.6 copy-start.7
  413.9 7.6 %copy-start.6 = (f32[3200]{0:T(1024)S(1)}, f32[3200]{0:T(1024)}, u32[]{:S(2)}) copy-start(f32[3200]{0:T(1024)} %param.33) | copy-start | bytes 38404
  530.1 10.3 %copy-start = (s32[800,5120]{1,0:T(8,128)S(1)}, s32[800,5120]{1,0:T(8,128)}, u32[]{:S(2)}) copy-start(s32[800,5120]{1,0:T(8,128)} %all-gather.8.cloned.1.call-done) | copy-start | bytes 49152004
  542.9 2.5 copy-start.3
Sparse Core Ops, SparseCore 0:
  85.8 46.4 all-reduce.1
  548.4 23.8 reduce-scatter.1
Sparse Core Ops, SparseCore 1:
  87.8 147.4 all-gather.3
  236.7 145.9 all-gather.5
  384.2 145.9 all-gather.7
where the time goes:
time: 589 us; the launch traced here: 582 us
  waiting for transfers between devices  376 us (64%)
  matrix products  85.7 us (15%)
  local copies, waits for them, and re-layouts  82.3 us (14%)
  between operations  16.1 us (3%)
  blocking collectives  9.25 us (2%)
  other arithmetic  7.26 us (1%)
    all_gather x1, waiting for transfers between devices, local(): lax.all_gather(w_up, ('grp', 'src'), axis=0, tiled=True)  139 us
    all_gather x1, waiting for transfers between devices, local(): lax.all_gather(w_down, ('grp', 'src'), axis=1, tiled=True)  91.5 us
    dot_general x20, matrix products, byte_product(): jnp.dot(activations[:, byte_index::4], unpack_bytes(packed, byte_index).a...  81.8 us
    all_gather x1, waiting for transfers between devices, local(): lax.all_gather(w_gate, ('grp', 'src'), axis=0, tiled=True)  74.5 us
    slice x16, local copies, waits for them, and re-layouts, byte_product(): activations[:, byte_index::4]  72.7 us
    psum x1, waiting for transfers between devices, local(): lax.psum(partial_value.astype(jnp.bfloat16), 'tp').astype(jnp.float32)  44.9 us
    reduce_scatter x1, waiting for transfers between devices, local(): lax.psum_scatter(down_terms.astype(jnp.bfloat16), 'tp', scatter_dimension...  24 us
  transfers between devices with their start and end apart: 6, of which 5 were waited for; matrix products, arithmetic and copies ran while one was open for 17% of the time, Pallas kernels for 0%

commit v1 on v0

--- a/solution.py
+++ b/solution.py
@@ -1,8 +1,11 @@
+import functools
 import math
 
 import jax
 import jax.numpy as jnp
 from jax import lax
+from jax.experimental import pallas as pl
+from jax.experimental.pallas import tpu as pltpu
 from jax.sharding import PartitionSpec as P
 
 D = 5120
@@ -21,16 +24,88 @@
     return jnp.right_shift(jnp.left_shift(packed, 24 - 8 * byte_index), 24)
 
 
+def byte_order(block):
+    source = lax.broadcasted_iota(jnp.int32, (block, block), 0)
+    target = lax.broadcasted_iota(jnp.int32, (block, block), 1)
+    return (target == (source % 4) * (block // 4) + source // 4).astype(jnp.bfloat16)
+
+
+def split_kernel(block, x_ref, order_ref, out_ref):
+    lanes = block // 4
+    for c in range(x_ref.shape[1] // block):
+        moved = jnp.dot(
+            x_ref[:, c * block : (c + 1) * block],
+            order_ref[...],
+            preferred_element_type=jnp.float32,
+        ).astype(jnp.bfloat16)
+        for j in range(4):
+            out_ref[j, :, c * lanes : (c + 1) * lanes] = moved[:, j * lanes : (j + 1) * lanes]
+
+
+def split_bytes(activations):
+    rows, width = activations.shape
+    if width % 512:
+        return [activations[:, byte_index::4] for byte_index in range(4)]
+    split = pl.pallas_call(
+        functools.partial(split_kernel, 512),
+        out_shape=jax.ShapeDtypeStruct((4, rows, width // 4), jnp.bfloat16),
+        cost_estimate=pl.CostEstimate(
+            flops=2 * rows * width * 512, bytes_accessed=4 * rows * width, transcendentals=0
+        ),
+        name="split_bytes",
+    )(activations, byte_order(512))
+    return [split[byte_index] for byte_index in range(4)]
+
+
 def byte_product(activations, packed):
+    pieces = split_bytes(activations)
     products = [
         jnp.dot(
-            activations[:, byte_index::4],
+            pieces[byte_index],
             unpack_bytes(packed, byte_index).astype(jnp.bfloat16),
             preferred_element_type=jnp.float32,
         )
         for byte_index in range(4)
     ]
     return products[0] + products[1] + products[2] + products[3]
+
+
+def block_of(width):
+    return math.gcd(640, width)
+
+
+def order_kernel(block, x_ref, order_ref, out_ref):
+    for c in range(x_ref.shape[1] // block):
+        out_ref[:, c * block : (c + 1) * block] = jnp.dot(
+            x_ref[:, c * block : (c + 1) * block],
+            order_ref[...],
+            preferred_element_type=jnp.float32,
+        ).astype(jnp.bfloat16)
+
+
+def order_bytes(activations):
+    rows, width = activations.shape
+    block = block_of(width)
+    if block == width:
+        return jnp.dot(activations, byte_order(block), preferred_element_type=jnp.float32).astype(
+            jnp.bfloat16
+        )
+    return pl.pallas_call(
+        functools.partial(order_kernel, block),
+        out_shape=jax.ShapeDtypeStruct((rows, width), jnp.bfloat16),
+        cost_estimate=pl.CostEstimate(
+            flops=2 * rows * width * block, bytes_accessed=4 * rows * width, transcendentals=0
+        ),
+        name="order_bytes",
+    )(activations, byte_order(block))
+
+
+def unpack_ordered(packed):
+    rows, columns = packed.shape
+    block = block_of(4 * rows) // 4
+    blocks = packed.reshape(rows // block, block, columns)
+    parts = [unpack_bytes(blocks, j).astype(jnp.bfloat16) for j in range(4)]
+    return jnp.stack(parts, axis=1).reshape(4 * rows, columns)
 
 
 def normalize_rows(values, gain_row):
@@ -113,6 +188,14 @@
         (numerator / denominator[..., None])
         .reshape(count_of_rows, QUERY_COLUMNS)
         .astype(jnp.bfloat16)
+    )
+
+
+def summed_share(terms, tp_count):
+    rows, columns = terms.shape
+    pieces = lax.all_to_all(terms, "tp", split_axis=1, concat_axis=0, tiled=True)
+    return jnp.sum(
+        pieces.reshape(tp_count, rows, columns // tp_count).astype(jnp.float32), axis=0
     )
 
 
@@ -147,23 +230,37 @@
         query_key_value_rows, q_gain, k_gain, key_cache[0], value_cache[0], lengths[0]
     )
     head_rows = lax.all_to_all(heads_out, "tp", split_axis=1, concat_axis=0, tiled=True)
-    partial_value = byte_product(head_rows, w_out) * out_scale
-    attn_full = lax.psum(partial_value.astype(jnp.bfloat16), "tp").astype(jnp.float32)
-    mid_full = (residual + attn_full).astype(jnp.bfloat16)
+    partial_value = (byte_product(head_rows, w_out) * out_scale).astype(jnp.bfloat16)
+    residual_share = lax.dynamic_slice_in_dim(hidden_in, tp_index * share_cols, share_cols, 1)
+    mid_share = (
+        residual_share.astype(jnp.float32) + summed_share(partial_value, tp_count)
+    ).astype(jnp.bfloat16)
+    mid_full = lax.all_gather(mid_share, "tp", axis=1, tiled=True)
     normed_mlp = normalize_rows(mid_full.astype(jnp.float32), mlp_gain).astype(jnp.bfloat16)
-    mid_share = lax.dynamic_slice_in_dim(mid_full, tp_index * share_cols, share_cols, 1)
-    gate_total = byte_product(
-        normed_mlp, lax.all_gather(w_gate, ("grp", "src"), axis=0, tiled=True)
-    )
-    up_total = byte_product(normed_mlp, lax.all_gather(w_up, ("grp", "src"), axis=0, tiled=True))
-    activated = (jax.nn.silu(gate_total * gate_scale) * (up_total * up_scale)).astype(jnp.bfloat16)
-    down_terms = (
-        byte_product(activated, lax.all_gather(w_down, ("grp", "src"), axis=1, tiled=True))
-        * down_scale
-    )
-    mlp_share = lax.psum_scatter(
-        down_terms.astype(jnp.bfloat16), "tp", scatter_dimension=1, tiled=True
-    ).astype(jnp.float32)
+    mlp_columns = order_bytes(
+        lax.all_to_all(normed_mlp, ("grp", "src"), split_axis=1, concat_axis=0, tiled=True)
+    )
+    gate_terms = jnp.dot(mlp_columns, unpack_ordered(w_gate), preferred_element_type=jnp.float32)
+    up_terms = jnp.dot(mlp_columns, unpack_ordered(w_up), preferred_element_type=jnp.float32)
+    both_terms = jnp.concatenate(
+        [gate_terms.astype(jnp.bfloat16), up_terms.astype(jnp.bfloat16)], axis=1
+    )
+    both = lax.psum_scatter(both_terms, ("grp", "src"), scatter_dimension=0, tiled=True).astype(
+        jnp.float32
+    )
+    hidden = gate_scale.shape[0]
+    gate_value = both[:, :hidden] * gate_scale
+    up_value = both[:, hidden:] * up_scale
+    activated = order_bytes((jax.nn.silu(gate_value) * up_value).astype(jnp.bfloat16))
+    all_activated = lax.all_gather(activated, ("grp", "src"), axis=0, tiled=True)
+    down_columns = jnp.dot(
+        all_activated, unpack_ordered(w_down), preferred_element_type=jnp.float32
+    ).astype(jnp.bfloat16)
+    down_rows = lax.all_to_all(
+        down_columns, ("grp", "src"), split_axis=0, concat_axis=1, tiled=True
+    )
+    down_share = lax.dynamic_slice_in_dim(down_scale, tp_index * share_cols, share_cols, 0)
+    mlp_share = summed_share(down_rows, tp_count) * down_share
     return (mid_share.astype(jnp.float32) + mlp_share).astype(jnp.bfloat16)
 
 

time: 589 us -> 350 us (0.59); the launches traced: 582 us -> 349 us
  waiting for transfers between devices: 376 us -> 191 us
  local copies, waits for them, and re-layouts: 82.3 us -> 13.2 us
  matrix products: 85.7 us -> 35.4 us
  other arithmetic: 7.26 us -> 33.5 us
  blocking collectives: 9.25 us -> 31.5 us
  starting transfers between devices: 5.49 us -> 22.3 us
  Pallas kernels: 0 us -> 7.99 us
    all_gather x3 -> x1, waiting for transfers between devices: 305 us -> 36.8 us  [local(): lax.all_gather(activated, ('grp', 'src'), axis=0, tiled=True)]
    reduce_scatter x1, waiting for transfers between devices: 24 us -> 129 us  [local(): lax.psum_scatter(both_terms, ('grp', 'src'), scatter_dimension=0, tiled=T...]
    slice x16 -> x0, local copies, waits for them, and re-layouts: 72.7 us -> none  [byte_product(): activations[:, byte_index::4]]
    dot_general x20 -> x12, matrix products: 81.8 us -> 31.5 us  [the longest x8 17.2 us: byte_product(): jnp.dot(pieces[byte_index], unpack_bytes(packed, byte_index).astype(jnp.b...]
    psum x1 -> x0, waiting for transfers between devices: 44.9 us -> none  [local(): lax.psum(partial_value.astype(jnp.bfloat16), 'tp').astype(jnp.float32)]
    all_to_all x0 -> x4, waiting for transfers between devices: none -> 25.9 us  [the longest x2 12.4 us: summed_share(): lax.all_to_all(terms, 'tp', split_axis=1, concat_axis=0, tiled=True)]
    all_to_all x0 -> x4, starting transfers between devices: none -> 17.1 us  [the longest x2 8 us: summed_share(): lax.all_to_all(terms, 'tp', split_axis=1, concat_axis=0, tiled=True)]
    another operation x1 -> x6, other arithmetic: 0.09 us -> 15.6 us  [the longest x5 15.5 us: unpack_ordered(): return jnp.stack(parts, axis=1).reshape(4 * rows, columns)]
  transfers between devices with their start and end apart: 6 -> 7, of which waited for: 5 -> 6; matrix products, arithmetic and copies ran while one was open for 17% -> 7% of each run, Pallas kernels for 0% -> 0%
where the time goes in v1:
time: 350 us; the launch traced here: 349 us
  waiting for transfers between devices  191 us (55%)
  matrix products  35.4 us (10%)
  other arithmetic  33.5 us (10%)
  blocking collectives  31.5 us (9%)
  starting transfers between devices  22.3 us (6%)
  between operations  13.9 us (4%)
  local copies, waits for them, and re-layouts  13.2 us (4%)
  Pallas kernels  7.99 us (2%)
    reduce_scatter x1, waiting for transfers between devices, local(): lax.psum_scatter(both_terms, ('grp', 'src'), scatter_dimension=0, tiled=T...  129 us
    all_gather x1, waiting for transfers between devices, local(): lax.all_gather(activated, ('grp', 'src'), axis=0, tiled=True)  36.8 us
    all_to_all x1, blocking collectives, local(): lax.all_to_all(down_columns, ('grp', 'src'), split_axis=0, concat_axis=1,...  20.4 us
    dot_general x8, matrix products, byte_product(): jnp.dot(pieces[byte_index], unpack_bytes(packed, byte_index).astype(jnp.b...  17.2 us
    another operation x5, other arithmetic, unpack_ordered(): return jnp.stack(parts, axis=1).reshape(4 * rows, columns)  15.5 us
    all_to_all x2, waiting for transfers between devices, summed_share(): lax.all_to_all(terms, 'tp', split_axis=1, concat_axis=0, tiled=True)  12.4 us
    all_to_all x1, waiting for transfers between devices, local(): lax.all_to_all(normed_mlp, ('grp', 'src'), split_axis=1, concat_axis=0, t...  11.9 us
    all_gather x1, blocking collectives, local(): mid_full = lax.all_gather(mid_share, 'tp', axis=1, tiled=True)  11.1 us
  transfers between devices with their start and end apart: 7, of which 6 were waited for; matrix products, arithmetic and copies ran while one was open for 7% of the time, Pallas kernels for 0%

profile of v1, /device:TPU:0, one launch (start us, length us, event | category | flops | bytes accessed | tf_op | source)
XLA Modules:
  0.0 349.1 jit_solution(6845188999619874893)
XLA Ops:
  7.9 2.2 fusion.32.x_ref
  11.4 3.1 split_bytes.2
  14.5 4.1 %fusion.2 = f32[64,1280]{1,0:T(8,128)S(1)} fusion(s32[1280,1280]{1,0:T(8,128)} %param.20, bf16[4,64,1280]{2,1,0:T(8,128)(2,1)} %split_bytes.2), kind=kOutput, calls=%fused_computation.19 | convolution fusion | flops 214630400 | bytes 7045120 | tf_op jit(solution)/shard_map/dot_general | solution.py:63
  23.9 5.2 %all-to-all-start = ((bf16[4,16,1280]{2,1,0:T(8,128)(2,1)}), bf16[4,16,1280]{2,1,0:T(8,128)(2,1)S(1)}, u32[]{:S(2)}, u32[]{:S(2)}) async-start(bf16[4,16,1280]{2,1,0:T(8,128)(2,1)} %bitcast.5), calls=%async_computation | async-start | bytes 327680 | tf_op jit(solution)/shard_map/all_to_all | solution.py:228
  29.1 2.6 reshape_squeeze.6
  31.7 4.0 %reshape_squeeze.7 = bf16[16,128,4,128]{3,2,1,0:T(4,128)(2,1)} reshape(bf16[1,16,128,512]{3,2,1,0:T(8,128)(2,1)} %param.25) | data formatting | bytes 4194304 | tf_op jit(solution)/shard_map/reshape;squeeze | solution.py:163
  38.9 2.3 fusion.48
  41.9 4.2 %all-to-all-start.1 = ((bf16[16,4,1024]{2,0,1:T(8,128)(2,1)}), bf16[16,4,1024]{2,0,1:T(8,128)(2,1)S(1)}, u32[]{:S(2)}, u32[]{:S(2)}) async-start(bf16[16,4,1024]{2,0,1:T(8,128)(2,1)} %copy.36), calls=%async_computation.1 | async-start | bytes 262144 | tf_op jit(solution)/shard_map/all_to_all | solution.py:232
  46.1 3.4 fusion.52
  51.8 2.1 split_bytes.3
  53.8 3.5 fusion.13
  57.4 3.5 convolution_add_fusion.2
  63.4 4.3 %all-to-all-start.2 = ((bf16[64,4,1280]{2,0,1:T(8,128)(2,1)}), bf16[64,4,1280]{2,0,1:T(8,128)(2,1)}, u32[]{:S(2)}, u32[]{:S(2)}) async-start(bf16[64,4,1280]{2,0,1:T(8,128)(2,1)} %bitcast.104), calls=%async_computation.2 | async-start | bytes 1310720 | tf_op jit(solution)/shard_map/all_to_all | solution.py:196
  67.8 4.2 %fusion.56 = (bf16[1,1,160,3200]{3,2,1,0:T(8,128)(2,1)}, bf16[1,1,160,3200]{3,2,1,0:T(8,128)(2,1)}, bf16[1,1,160,3200]{3,2,1,0:T(8,128)(2,1)}, bf16[1,1,160,3200]{3,2,1,0:T(8,128)(2,1)}) fusion(s32[160,3200]{1,0:T(8,128)} %param.31), kind=kLoop, calls=%fused_computation.85 | loop fusion | flops 6144000 | bytes 6144000 | tf_op jit(solution)/shard_map/stack | solution.py:108
  72.0 3.4 all-to-all-done.2
  77.6 11.1 %all_gather.6 = bf16[64,5120]{1,0:T(8,128)(2,1)S(1)} all-gather(bf16[64,1280]{1,0:T(8,128)(2,1)S(1)} %add_convert_fusion.1), channel_id=1, replica_groups=mesh['grp'=2,'tp'=4,'src'=4] {'tp'}, dimensions={1}, use_global_device_ids=true | all-gather | bytes 819200 | tf_op jit(solution)/shard_map/all_gather | solution.py:238
  90.1 4.9 %all-to-all-start.3 = ((bf16[64,8,640]{2,0,1:T(8,128)(2,1)}), bf16[64,8,640]{2,0,1:T(8,128)(2,1)}, u32[]{:S(2)}, u32[]{:S(2)}) async-start(bf16[64,8,640]{2,0,1:T(8,128)(2,1)} %bitcast.105), calls=%async_computation.3 | async-start | bytes 1310720 | tf_op jit(solution)/shard_map/all_to_all | solution.py:241
  95.1 3.4 pad_maximum_fusion.1
  98.5 2.3 pad_maximum_fusion.2
  100.8 11.9 %all-to-all-done.3 = bf16[64,8,640]{2,0,1:T(8,128)(2,1)} async-done(((bf16[64,8,640]{2,0,1:T(8,128)(2,1)}), bf16[64,8,640]{2,0,1:T(8,128)(2,1)}, u32[]{:S(2)}, u32[]{:S(2)}) %all-to-all-start.3) | async-done | bytes 655392 | tf_op jit(solution)/shard_map/all_to_all | solution.py:241
  112.6 2.4 convolution_convert_fusion.2
  115.0 3.0 convolution_convert_fusion.1
  118.1 3.0 convolution_convert_fusion
  121.1 3.2 pad_maximum_fusion
  126.4 128.5 %reduce-scatter.2.cloned.1.call-done = bf16[64,6400]{1,0:T(8,128)(2,1)} async-done(((bf16[512,6400]{1,0:T(8,128)(2,1)}), bf16[64,6400]{1,0:T(8,128)(2,1)}) %reduce-scatter.2.cloned.1.call-update) | async-done | bytes 819216 | tf_op jit(solution)/shard_map/reduce_scatter | solution.py:248
  257.2 2.8 order_bytes.1
  261.0 2.2 pad_maximum_fusion.3
  263.2 36.8 %all-gather.2.cloned.1.call-done = bf16[512,3200]{1,0:T(8,128)(2,1)} async-done(((bf16[64,3200]{1,0:T(8,128)(2,1)}), bf16[512,3200]{1,0:T(8,128)(2,1)}) %all-gather.2.cloned.1.call-update) | async-done | bytes 3276816 | tf_op jit(solution)/shard_map/all_gather | solution.py:255
  300.1 5.9 %convolution_convert_fusion.3 = bf16[512,640]{1,0:T(8,128)(2,1)S(1)} fusion(bf16[512,3200]{1,0:T(8,128)(2,1)} %all-gather.2.cloned.1.call-done, bf16[3200,640]{1,0:T(8,128)(2,1)} %bitcast.98), kind=kOutput, calls=%fused_computation.65 | convolution fusion | flops 2097479680 | bytes 8028160 | tf_op jit(solution)/shard_map/dot_general | solution.py:256
  306.0 20.4 %all_to_all.96 = bf16[8,64,640]{2,1,0:T(8,128)(2,1)S(1)} all-to-all(bf16[8,64,640]{2,1,0:T(8,128)(2,1)S(1)} %bitcast.111), channel_id=1, replica_groups=mesh['grp'=2,'tp'=4,'src'=4] {'grp','src'}, dimensions={0} | all-to-all | bytes 1310720 | tf_op jit(solution)/shard_map/all_to_all | solution.py:259
  328.1 3.6 %all-to-all-start.5 = ((bf16[64,4,1280]{2,0,1:T(8,128)(2,1)}), bf16[64,4,1280]{2,0,1:T(8,128)(2,1)S(1)}, u32[]{:S(2)}, u32[]{:S(2)}) async-start(bf16[64,4,1280]{2,0,1:T(8,128)(2,1)} %copy.40), calls=%async_computation.6 | async-start | bytes 1310720 | tf_op jit(solution)/shard_map/all_to_all | solution.py:196
  332.5 9.0 %all-to-all-done.5 = bf16[64,4,1280]{2,0,1:T(8,128)(2,1)S(1)} async-done(((bf16[64,4,1280]{2,0,1:T(8,128)(2,1)}), bf16[64,4,1280]{2,0,1:T(8,128)(2,1)S(1)}, u32[]{:S(2)}, u32[]{:S(2)}) %all-to-all-start.5) | async-done | bytes 655392 | tf_op jit(solution)/shard_map/all_to_all | solution.py:196
  (107 shorter events, 28.8 us)
Async XLA Ops:
  14.5 4.8 %copy-start = (s32[1280,1280]{1,0:T(8,128)S(1)}, s32[1280,1280]{1,0:T(8,128)}, u32[]{:S(2)}) copy-start(s32[1280,1280]{1,0:T(8,128)} %param.20) | copy-start | bytes 19660804
  19.3 2.0 copy-start.7
  21.3 1.0 copy-start.15
  22.4 6.7 %copy-start.18 = (s32[1,16]{1,0:T(1,128)S(1)}, s32[1,16]{1,0:T(1,128)}, u32[]{:S(2)}) copy-start(s32[1,16]{1,0:T(1,128)} %param.26) | copy-start | bytes 196
  23.9 12.0 %all-to-all-start = ((bf16[4,16,1280]{2,1,0:T(8,128)(2,1)}), bf16[4,16,1280]{2,1,0:T(8,128)(2,1)S(1)}, u32[]{:S(2)}, u32[]{:S(2)}) async-start(bf16[4,16,1280]{2,1,0:T(8,128)(2,1)} %bitcast.5), calls=%async_computation | async-start | bytes 327680 | tf_op jit(solution)/shard_map/all_to_all | solution.py:228
  31.7 4.6 %copy-start.16 = (f32[128]{0:T(128)S(1)}, f32[128]{0:T(128)}, u32[]{:S(2)}) copy-start(f32[128]{0:T(128)} %param.23) | copy-start | bytes 1540
  31.7 4.7 %copy-start.17 = (f32[128]{0:T(128)S(1)}, f32[128]{0:T(128)}, u32[]{:S(2)}) copy-start(f32[128]{0:T(128)} %param.22) | copy-start | bytes 1540
  41.9 9.2 %all-to-all-start.1 = ((bf16[16,4,1024]{2,0,1:T(8,128)(2,1)}), bf16[16,4,1024]{2,0,1:T(8,128)(2,1)S(1)}, u32[]{:S(2)}, u32[]{:S(2)}) async-start(bf16[16,4,1024]{2,0,1:T(8,128)(2,1)} %copy.36), calls=%async_computation.1 | async-start | bytes 262144 | tf_op jit(solution)/shard_map/all_to_all | solution.py:232
  51.1 0.7 copy-start.10
  53.8 3.5 %copy-start.9 = (bf16[4,64,256]{2,1,0:T(8,128)(2,1)S(1)}, bf16[4,64,256]{2,1,0:T(8,128)(2,1)}, u32[]{:S(2)}) copy-start(bf16[4,64,256]{2,1,0:T(8,128)(2,1)} %split_bytes.3) | copy-start | bytes 393220
  53.8 7.0 %slice-start = ((s8[5242880]{0:T(1024)(128)(4,1)}), s8[4194304]{0:T(1024)(128)(4,1)S(1)}, s32[]{:S(2)}) async-start(s8[5242880]{0:T(1024)(128)(4,1)} %bitcast.94), calls=%async_computation.9 | async-start | bytes 8388608
  57.3 3.5 %slice-start.1 = ((s8[5242880]{0:T(1024)(128)(4,1)}), s8[1048576]{0:T(1024)(128)(4,1)S(1)}, s32[]{:S(2)}) async-start(s8[5242880]{0:T(1024)(128)(4,1)} %bitcast.94), calls=%async_computation.10 | async-start | bytes 2097152
  60.9 0.9 copy-start.11
  63.4 12.0 %all-to-all-start.2 = ((bf16[64,4,1280]{2,0,1:T(8,128)(2,1)}), bf16[64,4,1280]{2,0,1:T(8,128)(2,1)}, u32[]{:S(2)}, u32[]{:S(2)}) async-start(bf16[64,4,1280]{2,0,1:T(8,128)(2,1)} %bitcast.104), calls=%async_computation.2 | async-start | bytes 1310720 | tf_op jit(solution)/shard_map/all_to_all | solution.py:196
  71.9 17.0 %copy-start.12 = (f32[5120]{0:T(1024)S(1)}, f32[5120]{0:T(1024)}, u32[]{:S(2)}) copy-start(f32[5120]{0:T(1024)} %param.29) | copy-start | bytes 61444
  90.1 22.5 %all-to-all-start.3 = ((bf16[64,8,640]{2,0,1:T(8,128)(2,1)}), bf16[64,8,640]{2,0,1:T(8,128)(2,1)}, u32[]{:S(2)}, u32[]{:S(2)}) async-start(bf16[64,8,640]{2,0,1:T(8,128)(2,1)} %bitcast.105), calls=%async_computation.3 | async-start | bytes 1310720 | tf_op jit(solution)/shard_map/all_to_all | solution.py:241
  95.0 159.9 %reduce-scatter.2.cloned.1.call-start = ((), (), s32[]{:S(2)}) async-start(), calls=%async_computation.7 | async-start | bytes 7372800 | tf_op jit(solution)/shard_map/reduce_scatter | solution.py:248
  95.0 3.4 copy-start.3
  95.0 3.4 copy-start.4
  95.0 3.4 copy-start.5
  95.0 3.4 copy-start.6
  112.6 2.4 copy-start.1
  115.0 3.0 copy-start.2
  124.3 131.8 %copy-start.13 = (f32[3200]{0:T(1024)S(1)}, f32[3200]{0:T(1024)}, u32[]{:S(2)}) copy-start(f32[3200]{0:T(1024)} %param.33) | copy-start | bytes 38404
  124.3 131.8 %copy-start.14 = (f32[3200]{0:T(1024)S(1)}, f32[3200]{0:T(1024)}, u32[]{:S(2)}) copy-start(f32[3200]{0:T(1024)} %param.32) | copy-start | bytes 38404
  124.3 175.7 %all-gather.2.cloned.1.call-start = ((), (), s32[]{:S(2)}) async-start(), calls=%async_computation.8 | async-start | bytes 3686400 | tf_op jit(solution)/shard_map/all_gather | solution.py:255
  256.2 3.8 %copy-start.8 = (s32[800,640]{1,0:T(8,128)S(1)}, s32[800,640]{1,0:T(8,128)}, u32[]{:S(2)}) copy-start(s32[800,640]{1,0:T(8,128)} %param.34) | copy-start | bytes 6144004
  328.1 13.4 %all-to-all-start.5 = ((bf16[64,4,1280]{2,0,1:T(8,128)(2,1)}), bf16[64,4,1280]{2,0,1:T(8,128)(2,1)S(1)}, u32[]{:S(2)}, u32[]{:S(2)}) async-start(bf16[64,4,1280]{2,0,1:T(8,128)(2,1)} %copy.40), calls=%async_computation.6 | async-start | bytes 1310720 | tf_op jit(solution)/shard_map/all_to_all | solution.py:196
Sparse Core Ops, SparseCore 0:
  124.4 130.4 reduce-scatter.1
  260.1 39.9 all-gather.1

commit v2 on v1

--- a/solution.py
+++ b/solution.py
@@ -197,6 +197,22 @@
     return jnp.sum(
         pieces.reshape(tp_count, rows, columns // tp_count).astype(jnp.float32), axis=0
     )
+
+
+def gathered_rows(rows, axis):
+    count = lax.axis_size(axis)
+    copies = jnp.broadcast_to(rows[None], (count, *rows.shape))
+    pieces = lax.all_to_all(copies, axis, split_axis=0, concat_axis=0)
+    return pieces.reshape(count * rows.shape[0], rows.shape[1])
+
+
+def summed_rows(terms, axis):
+    count = lax.axis_size(axis)
+    rows, columns = terms.shape
+    pieces = lax.all_to_all(
+        terms.reshape(count, rows // count, columns), axis, split_axis=0, concat_axis=0
+    )
+    return jnp.sum(pieces.astype(jnp.float32), axis=0)
 
 
 def local(
@@ -245,14 +261,12 @@
     both_terms = jnp.concatenate(
         [gate_terms.astype(jnp.bfloat16), up_terms.astype(jnp.bfloat16)], axis=1
     )
-    both = lax.psum_scatter(both_terms, ("grp", "src"), scatter_dimension=0, tiled=True).astype(
-        jnp.float32
-    )
+    both = summed_rows(summed_rows(both_terms, "grp").astype(jnp.bfloat16), "src")
     hidden = gate_scale.shape[0]
     gate_value = both[:, :hidden] * gate_scale
     up_value = both[:, hidden:] * up_scale
     activated = order_bytes((jax.nn.silu(gate_value) * up_value).astype(jnp.bfloat16))
-    all_activated = lax.all_gather(activated, ("grp", "src"), axis=0, tiled=True)
+    all_activated = gathered_rows(gathered_rows(activated, "src"), "grp")
     down_columns = jnp.dot(
         all_activated, unpack_ordered(w_down), preferred_element_type=jnp.float32
     ).astype(jnp.bfloat16)

time: 350 us -> 308 us (0.88)
  waiting for transfers between devices: 191 us -> 131 us
  blocking collectives: 31.5 us -> 48.4 us
  between operations: 13.9 us -> 0.53 us
  starting transfers between devices: 22.3 us -> 29.6 us
  other arithmetic: 33.5 us -> 40.1 us
    reduce_scatter x1 -> x0, waiting for transfers between devices: 129 us -> none  [local(): lax.psum_scatter(both_terms, ('grp', 'src'), scatter_dimension=0, tiled=T...]
    all_to_all x0 -> x2, waiting for transfers between devices: none -> 105 us  [the longest x1 72 us: summed_rows(): lax.all_to_all(terms.reshape(count, rows // count, columns), axis, split_...]
    all_gather x1 -> x0, waiting for transfers between devices: 36.8 us -> none  [local(): lax.all_gather(activated, ('grp', 'src'), axis=0, tiled=True)]
    all_to_all x0 -> x2, blocking collectives: none -> 16.8 us  [the longest x1 10.2 us: summed_rows(): lax.all_to_all(terms.reshape(count, rows // count, columns), axis, split_...]
    all_to_all x0 -> x2, starting transfers between devices: none -> 7.5 us  [the longest x1 3.79 us: gathered_rows(): pieces = lax.all_to_all(copies, axis, split_axis=0, concat_axis=0)]
    reduce_sum x0 -> x2, other arithmetic: none -> 7.09 us  [summed_rows(): return jnp.sum(pieces.astype(jnp.float32), axis=0)]
  transfers between devices with their start and end apart: 7 -> 7, of which waited for: 6 -> 6; matrix products, arithmetic and copies ran while one was open for 7% -> 9% of each run, Pallas kernels for 0% -> 0%
where the time goes in v2:
time: 308 us; the launch traced here: 307 us
  waiting for transfers between devices  131 us (43%)
  blocking collectives  48.4 us (16%)
  other arithmetic  40.1 us (13%)
  matrix products  33.5 us (11%)
  starting transfers between devices  29.6 us (10%)
  local copies, waits for them, and re-layouts  15.7 us (5%)
  Pallas kernels  7.98 us (3%)
    all_to_all x1, waiting for transfers between devices, summed_rows(): lax.all_to_all(terms.reshape(count, rows // count, columns), axis, split_...  72 us
    all_to_all x1, waiting for transfers between devices, gathered_rows(): pieces = lax.all_to_all(copies, axis, split_axis=0, concat_axis=0)  33 us
    all_to_all x1, blocking collectives, local(): lax.all_to_all(down_columns, ('grp', 'src'), split_axis=0, concat_axis=1,...  20.5 us
    dot_general x8, matrix products, byte_product(): jnp.dot(pieces[byte_index], unpack_bytes(packed, byte_index).astype(jnp.b...  17.2 us
    another operation x5, other arithmetic, unpack_ordered(): return jnp.stack(parts, axis=1).reshape(4 * rows, columns)  15.5 us
    all_to_all x2, waiting for transfers between devices, summed_share(): lax.all_to_all(terms, 'tp', split_axis=1, concat_axis=0, tiled=True)  12.6 us
    all_to_all x1, waiting for transfers between devices, local(): lax.all_to_all(normed_mlp, ('grp', 'src'), split_axis=1, concat_axis=0, t...  11.9 us
    all_gather x1, blocking collectives, local(): mid_full = lax.all_gather(mid_share, 'tp', axis=1, tiled=True)  11.1 us
  transfers between devices with their start and end apart: 7, of which 6 were waited for; matrix products, arithmetic and copies ran while one was open for 9% of the time, Pallas kernels for 0%

profile of v2, /device:TPU:0, one launch (start us, length us, event | category | flops | bytes accessed | tf_op | source)
XLA Modules:
  0.0 307.0 jit_solution(5775638950331051432)
XLA Ops:
  4.8 3.1 %split_bytes.2 = bf16[4,64,1280]{2,1,0:T(8,128)(2,1)} custom-call(bf16[64,5120]{1,0:T(8,128)(2,1)} %fusion.32.x_ref, bf16[512,512]{1,0:T(8,128)(2,1)} %fusion.51.order_ref), custom_call_target="tpu_custom_call" | custom-call | flops 335544320 | bytes 1310720 | tf_op jit(solution)/shard_map/split_bytes/pallas_call | solution.py:49
  7.9 4.1 %fusion.2 = f32[64,1280]{1,0:T(8,128)S(1)} fusion(s32[1280,1280]{1,0:T(8,128)} %param.20, bf16[4,64,1280]{2,1,0:T(8,128)(2,1)} %split_bytes.2), kind=kOutput, calls=%fused_computation.20 | convolution fusion | flops 214630400 | bytes 7045120 | tf_op jit(solution)/shard_map/dot_general | solution.py:63
  17.3 5.2 %all-to-all-start = ((bf16[4,16,1280]{2,1,0:T(8,128)(2,1)}), bf16[4,16,1280]{2,1,0:T(8,128)(2,1)S(1)}, u32[]{:S(2)}, u32[]{:S(2)}) async-start(bf16[4,16,1280]{2,1,0:T(8,128)(2,1)} %bitcast.5), calls=%async_computation | async-start | bytes 327680 | tf_op jit(solution)/shard_map/all_to_all | solution.py:244
  22.6 2.6 reshape_squeeze.6
  25.2 4.0 %reshape_squeeze.7 = bf16[16,128,4,128]{3,2,1,0:T(4,128)(2,1)} reshape(bf16[1,16,128,512]{3,2,1,0:T(8,128)(2,1)} %param.25) | data formatting | bytes 4194304 | tf_op jit(solution)/shard_map/reshape;squeeze | solution.py:163
  35.4 4.2 %all-to-all-start.1 = ((bf16[16,4,1024]{2,0,1:T(8,128)(2,1)}), bf16[16,4,1024]{2,0,1:T(8,128)(2,1)S(1)}, u32[]{:S(2)}, u32[]{:S(2)}) async-start(bf16[16,4,1024]{2,0,1:T(8,128)(2,1)} %copy.44), calls=%async_computation.1 | async-start | bytes 262144 | tf_op jit(solution)/shard_map/all_to_all | solution.py:248
  39.6 3.4 %fusion.52 = (bf16[1,1,160,3200]{3,2,1,0:T(8,128)(2,1)S(1)}, bf16[1,1,160,3200]{3,2,1,0:T(8,128)(2,1)S(1)}, bf16[1,1,160,3200]{3,2,1,0:T(8,128)(2,1)S(1)}, bf16[1,1,160,3200]{3,2,1,0:T(8,128)(2,1)}) fusion(s32[160,3200]{1,0:T(8,128)} %param.30), kind=kLoop, calls=%fused_computation.82 | loop fusion | flops 6144000 | bytes 6144000 | tf_op jit(solution)/shard_map/stack | solution.py:108
  47.3 3.5 %fusion.13 = f32[64,5120]{1,0:T(8,128)S(1)} fusion(s32[256,5120]{1,0:T(8,128)} %param.27, bf16[4,64,256]{2,1,0:T(8,128)(2,1)} %split_bytes.3), kind=kOutput, calls=%fused_computation.31 | convolution fusion | flops 171704320 | bytes 6586368 | tf_op jit(solution)/shard_map/dot_general | solution.py:63
  50.8 3.5 %convolution_add_fusion.2 = f32[64,5120]{1,0:T(8,128)S(1)} fusion(f32[64,5120]{1,0:T(8,128)S(1)} %fusion.13, s32[256,5120]{1,0:T(8,128)} %param.27, bf16[4,64,256]{2,1,0:T(8,128)(2,1)S(1)} %copy-done.9), kind=kOutput, calls=%fused_computation.10 | convolution fusion | flops 172032000 | bytes 7897088 | tf_op jit(solution)/shard_map/dot_general | solution.py:63
  56.9 4.3 %all-to-all-start.2 = ((bf16[64,4,1280]{2,0,1:T(8,128)(2,1)}), bf16[64,4,1280]{2,0,1:T(8,128)(2,1)}, u32[]{:S(2)}, u32[]{:S(2)}) async-start(bf16[64,4,1280]{2,0,1:T(8,128)(2,1)} %bitcast.112), calls=%async_computation.2 | async-start | bytes 1310720 | tf_op jit(solution)/shard_map/all_to_all | solution.py:196
  61.2 4.1 %fusion.56 = (bf16[1,1,160,3200]{3,2,1,0:T(8,128)(2,1)}, bf16[1,1,160,3200]{3,2,1,0:T(8,128)(2,1)}, bf16[1,1,160,3200]{3,2,1,0:T(8,128)(2,1)}, bf16[1,1,160,3200]{3,2,1,0:T(8,128)(2,1)}) fusion(s32[160,3200]{1,0:T(8,128)} %param.31), kind=kLoop, calls=%fused_computation.86 | loop fusion | flops 6144000 | bytes 6144000 | tf_op jit(solution)/shard_map/stack | solution.py:108
  65.4 3.5 %all-to-all-done.2 = bf16[64,4,1280]{2,0,1:T(8,128)(2,1)} async-done(((bf16[64,4,1280]{2,0,1:T(8,128)(2,1)}), bf16[64,4,1280]{2,0,1:T(8,128)(2,1)}, u32[]{:S(2)}, u32[]{:S(2)}) %all-to-all-start.2) | async-done | bytes 655392 | tf_op jit(solution)/shard_map/all_to_all | solution.py:196
  71.0 11.1 %all_gather.3 = bf16[64,5120]{1,0:T(8,128)(2,1)S(1)} all-gather(bf16[64,1280]{1,0:T(8,128)(2,1)S(1)} %add_convert_fusion.1), channel_id=1, replica_groups=mesh['grp'=2,'tp'=4,'src'=4] {'tp'}, dimensions={1}, use_global_device_ids=true | all-gather | bytes 819200 | tf_op jit(solution)/shard_map/all_gather | solution.py:254
  83.5 4.9 %all-to-all-start.3 = ((bf16[64,8,640]{2,0,1:T(8,128)(2,1)}), bf16[64,8,640]{2,0,1:T(8,128)(2,1)}, u32[]{:S(2)}, u32[]{:S(2)}) async-start(bf16[64,8,640]{2,0,1:T(8,128)(2,1)} %bitcast.113), calls=%async_computation.3 | async-start | bytes 1310720 | tf_op jit(solution)/shard_map/all_to_all | solution.py:257
  88.4 3.4 %pad_maximum_fusion.1 = bf16[1,4,160,3200]{3,2,1,0:T(8,128)(2,1)} fusion(bf16[1,1,160,3200]{3,2,1,0:T(8,128)(2,1)S(1)} %get-tuple-element.11, bf16[1,1,160,3200]{3,2,1,0:T(8,128)(2,1)} %get-tuple-element.12, bf16[1,1,160,3200]{3,2,1,0:T(8,128)(2,1)S(1)} %get-tuple-element.10, bf16[1,1,160,3200]{3,2,1,0:T(8,128)(2,1)S(1)} %get-tuple-element.9), kind=kLoop, calls=%fused_computation.17 | loop fusion | flops 6144000 | bytes 8192000 | tf_op jit(solution)/shard_map/stack | solution.py:108
  94.1 11.9 %all-to-all-done.3 = bf16[64,8,640]{2,0,1:T(8,128)(2,1)} async-done(((bf16[64,8,640]{2,0,1:T(8,128)(2,1)}), bf16[64,8,640]{2,0,1:T(8,128)(2,1)}, u32[]{:S(2)}, u32[]{:S(2)}) %all-to-all-start.3) | async-done | bytes 655392 | tf_op jit(solution)/shard_map/all_to_all | solution.py:257
  106.1 2.4 convolution_convert_fusion.2
  108.5 3.0 convolution_convert_fusion.1
  111.5 4.2 %convolution_convert_fusion = bf16[512,3200]{1,0:T(8,128)(2,1)} fusion(bf16[512,640]{1,0:T(8,128)(2,1)S(1)} %convolution_convert_fusion.2, bf16[640,3200]{1,0:T(8,128)(2,1)S(1)} %bitcast.104), kind=kOutput, calls=%fused_computation.6 | convolution fusion | flops 2098790400 | bytes 8028160 | tf_op jit(solution)/shard_map/dot_general | solution.py:260
  118.1 10.2 %all_to_all.116 = bf16[2,256,6400]{2,1,0:T(8,128)(2,1)} all-to-all(bf16[2,256,6400]{2,1,0:T(8,128)(2,1)S(1)} %bitcast.100), channel_id=1, replica_groups=mesh['grp'=2,'tp'=4,'src'=4] {'grp'}, dimensions={0} | all-to-all | bytes 13107200 | tf_op jit(solution)/shard_map/all_to_all | solution.py:212
  128.2 6.6 %reduce_sum.90 = bf16[256,6400]{1,0:T(8,128)(2,1)} reduce(bf16[2,256,6400]{2,1,0:T(8,128)(2,1)} %all_to_all.116, bf16[]{:T(256)} %constant.119.clone.1), dimensions={0}, to_apply=%region_7.8 | reduce | flops 1638400 | bytes 9830402 | tf_op jit(solution)/shard_map/reduce_sum | solution.py:215
  134.9 3.7 %all-to-all-start.5 = ((bf16[4,64,6400]{2,1,0:T(8,128)(2,1)}), bf16[4,64,6400]{2,1,0:T(8,128)(2,1)S(1)}, u32[]{:S(2)}, u32[]{:S(2)}) async-start(bf16[4,64,6400]{2,1,0:T(8,128)(2,1)} %bitcast.101), calls=%async_computation.5 | async-start | bytes 6553600 | tf_op jit(solution)/shard_map/all_to_all | solution.py:212
  140.6 72.0 %all-to-all-done.5 = bf16[4,64,6400]{2,1,0:T(8,128)(2,1)S(1)} async-done(((bf16[4,64,6400]{2,1,0:T(8,128)(2,1)}), bf16[4,64,6400]{2,1,0:T(8,128)(2,1)S(1)}, u32[]{:S(2)}, u32[]{:S(2)}) %all-to-all-start.5) | async-done | bytes 3276832 | tf_op jit(solution)/shard_map/all_to_all | solution.py:212
  214.1 2.8 order_bytes.1
  219.3 3.8 %all-to-all-start.6 = ((bf16[4,64,3200]{2,1,0:T(8,128)(2,1)}), bf16[4,64,3200]{2,1,0:T(8,128)(2,1)S(1)}, u32[]{:S(2)}, u32[]{:S(2)}) async-start(bf16[4,64,3200]{2,1,0:T(8,128)(2,1)} %broadcast_in_dim.16), calls=%async_computation.6 | async-start | bytes 3276800 | tf_op jit(solution)/shard_map/all_to_all | solution.py:205
  223.1 2.6 shift-right-arithmetic_convert_fusion.29
  227.9 33.0 %all-to-all-done.6 = bf16[4,64,3200]{2,1,0:T(8,128)(2,1)S(1)} async-done(((bf16[4,64,3200]{2,1,0:T(8,128)(2,1)}), bf16[4,64,3200]{2,1,0:T(8,128)(2,1)S(1)}, u32[]{:S(2)}, u32[]{:S(2)}) %all-to-all-start.6) | async-done | bytes 1638432 | tf_op jit(solution)/shard_map/all_to_all | solution.py:205
  261.1 6.6 %all_to_all.117 = bf16[2,256,3200]{2,1,0:T(8,128)(2,1)S(1)} all-to-all(bf16[2,256,3200]{2,1,0:T(8,128)(2,1)S(1)} %broadcast_in_dim.18), channel_id=1, replica_groups=mesh['grp'=2,'tp'=4,'src'=4] {'grp'}, dimensions={0} | all-to-all | bytes 6553600 | tf_op jit(solution)/shard_map/all_to_all | solution.py:205
  267.8 2.8 convolution_convert_fusion.3
  270.5 20.5 %all_to_all.118 = bf16[8,64,640]{2,1,0:T(8,128)(2,1)S(1)} all-to-all(bf16[8,64,640]{2,1,0:T(8,128)(2,1)S(1)} %bitcast.119), channel_id=1, replica_groups=mesh['grp'=2,'tp'=4,'src'=4] {'grp','src'}, dimensions={0} | all-to-all | bytes 1310720 | tf_op jit(solution)/shard_map/all_to_all | solution.py:273
  292.8 3.5 %all-to-all-start.9 = ((bf16[64,4,1280]{2,0,1:T(8,128)(2,1)}), bf16[64,4,1280]{2,0,1:T(8,128)(2,1)S(1)}, u32[]{:S(2)}, u32[]{:S(2)}) async-start(bf16[64,4,1280]{2,0,1:T(8,128)(2,1)} %copy.48), calls=%async_computation.9 | async-start | bytes 1310720 | tf_op jit(solution)/shard_map/all_to_all | solution.py:196
  297.0 9.2 %all-to-all-done.9 = bf16[64,4,1280]{2,0,1:T(8,128)(2,1)S(1)} async-done(((bf16[64,4,1280]{2,0,1:T(8,128)(2,1)}), bf16[64,4,1280]{2,0,1:T(8,128)(2,1)S(1)}, u32[]{:S(2)}, u32[]{:S(2)}) %all-to-all-start.9) | async-done | bytes 655392 | tf_op jit(solution)/shard_map/all_to_all | solution.py:196
  (110 shorter events, 42.9 us)
Async XLA Ops:
  7.9 4.8 %copy-start = (s32[1280,1280]{1,0:T(8,128)S(1)}, s32[1280,1280]{1,0:T(8,128)}, u32[]{:S(2)}) copy-start(s32[1280,1280]{1,0:T(8,128)} %param.20) | copy-start | bytes 19660804
  12.7 2.0 copy-start.8
  14.8 1.0 copy-start.15
  15.8 6.7 %copy-start.18 = (s32[1,16]{1,0:T(1,128)S(1)}, s32[1,16]{1,0:T(1,128)}, u32[]{:S(2)}) copy-start(s32[1,16]{1,0:T(1,128)} %param.26) | copy-start | bytes 196
  17.3 12.0 %all-to-all-start = ((bf16[4,16,1280]{2,1,0:T(8,128)(2,1)}), bf16[4,16,1280]{2,1,0:T(8,128)(2,1)S(1)}, u32[]{:S(2)}, u32[]{:S(2)}) async-start(bf16[4,16,1280]{2,1,0:T(8,128)(2,1)} %bitcast.5), calls=%async_computation | async-start | bytes 327680 | tf_op jit(solution)/shard_map/all_to_all | solution.py:244
  25.1 4.6 %copy-start.16 = (f32[128]{0:T(128)S(1)}, f32[128]{0:T(128)}, u32[]{:S(2)}) copy-start(f32[128]{0:T(128)} %param.23) | copy-start | bytes 1540
  25.1 4.7 %copy-start.17 = (f32[128]{0:T(128)S(1)}, f32[128]{0:T(128)}, u32[]{:S(2)}) copy-start(f32[128]{0:T(128)} %param.22) | copy-start | bytes 1540
  35.4 9.2 %all-to-all-start.1 = ((bf16[16,4,1024]{2,0,1:T(8,128)(2,1)}), bf16[16,4,1024]{2,0,1:T(8,128)(2,1)S(1)}, u32[]{:S(2)}, u32[]{:S(2)}) async-start(bf16[16,4,1024]{2,0,1:T(8,128)(2,1)} %copy.44), calls=%async_computation.1 | async-start | bytes 262144 | tf_op jit(solution)/shard_map/all_to_all | solution.py:248
  44.6 0.7 copy-start.10
  47.3 3.5 %copy-start.9 = (bf16[4,64,256]{2,1,0:T(8,128)(2,1)S(1)}, bf16[4,64,256]{2,1,0:T(8,128)(2,1)}, u32[]{:S(2)}) copy-start(bf16[4,64,256]{2,1,0:T(8,128)(2,1)} %split_bytes.3) | copy-start | bytes 393220
  47.3 7.0 %slice-start = ((s8[5242880]{0:T(1024)(128)(4,1)}), s8[4194304]{0:T(1024)(128)(4,1)S(1)}, s32[]{:S(2)}) async-start(s8[5242880]{0:T(1024)(128)(4,1)} %bitcast.98), calls=%async_computation.10 | async-start | bytes 8388608
  50.8 3.5 %slice-start.1 = ((s8[5242880]{0:T(1024)(128)(4,1)}), s8[1048576]{0:T(1024)(128)(4,1)S(1)}, s32[]{:S(2)}) async-start(s8[5242880]{0:T(1024)(128)(4,1)} %bitcast.98), calls=%async_computation.11 | async-start | bytes 2097152
  54.3 0.9 copy-start.11
  56.9 12.0 %all-to-all-start.2 = ((bf16[64,4,1280]{2,0,1:T(8,128)(2,1)}), bf16[64,4,1280]{2,0,1:T(8,128)(2,1)}, u32[]{:S(2)}, u32[]{:S(2)}) async-start(bf16[64,4,1280]{2,0,1:T(8,128)(2,1)} %bitcast.112), calls=%async_computation.2 | async-start | bytes 1310720 | tf_op jit(solution)/shard_map/all_to_all | solution.py:196
  65.3 17.0 %copy-start.12 = (f32[5120]{0:T(1024)S(1)}, f32[5120]{0:T(1024)}, u32[]{:S(2)}) copy-start(f32[5120]{0:T(1024)} %param.29) | copy-start | bytes 61444
  83.5 22.6 %all-to-all-start.3 = ((bf16[64,8,640]{2,0,1:T(8,128)(2,1)}), bf16[64,8,640]{2,0,1:T(8,128)(2,1)}, u32[]{:S(2)}, u32[]{:S(2)}) async-start(bf16[64,8,640]{2,0,1:T(8,128)(2,1)} %bitcast.113), calls=%async_computation.3 | async-start | bytes 1310720 | tf_op jit(solution)/shard_map/all_to_all | solution.py:257
  88.4 3.5 %copy-start.4 = (bf16[1,1,160,3200]{3,2,1,0:T(8,128)(2,1)S(1)}, bf16[1,1,160,3200]{3,2,1,0:T(8,128)(2,1)}, u32[]{:S(2)}) copy-start(bf16[1,1,160,3200]{3,2,1,0:T(8,128)(2,1)} %get-tuple-element.13) | copy-start | bytes 3072004
  88.4 3.5 %copy-start.5 = (bf16[1,1,160,3200]{3,2,1,0:T(8,128)(2,1)S(1)}, bf16[1,1,160,3200]{3,2,1,0:T(8,128)(2,1)}, u32[]{:S(2)}) copy-start(bf16[1,1,160,3200]{3,2,1,0:T(8,128)(2,1)} %get-tuple-element.14) | copy-start | bytes 3072004
  88.4 3.4 %copy-start.6 = (bf16[1,1,160,3200]{3,2,1,0:T(8,128)(2,1)S(1)}, bf16[1,1,160,3200]{3,2,1,0:T(8,128)(2,1)}, u32[]{:S(2)}) copy-start(bf16[1,1,160,3200]{3,2,1,0:T(8,128)(2,1)} %get-tuple-element.15) | copy-start | bytes 3072004
  88.4 3.4 %copy-start.7 = (bf16[1,1,160,3200]{3,2,1,0:T(8,128)(2,1)S(1)}, bf16[1,1,160,3200]{3,2,1,0:T(8,128)(2,1)}, u32[]{:S(2)}) copy-start(bf16[1,1,160,3200]{3,2,1,0:T(8,128)(2,1)} %get-tuple-element.16) | copy-start | bytes 3072004
  106.1 2.4 copy-start.1
  108.5 3.0 copy-start.2
  134.9 77.7 %all-to-all-start.5 = ((bf16[4,64,6400]{2,1,0:T(8,128)(2,1)}), bf16[4,64,6400]{2,1,0:T(8,128)(2,1)S(1)}, u32[]{:S(2)}, u32[]{:S(2)}) async-start(bf16[4,64,6400]{2,1,0:T(8,128)(2,1)} %bitcast.101), calls=%async_computation.5 | async-start | bytes 6553600 | tf_op jit(solution)/shard_map/all_to_all | solution.py:212
  140.6 72.5 %copy-start.13 = (f32[3200]{0:T(1024)S(1)}, f32[3200]{0:T(1024)}, u32[]{:S(2)}) copy-start(f32[3200]{0:T(1024)} %param.33) | copy-start | bytes 38404
  140.6 72.5 %copy-start.14 = (f32[3200]{0:T(1024)S(1)}, f32[3200]{0:T(1024)}, u32[]{:S(2)}) copy-start(f32[3200]{0:T(1024)} %param.32) | copy-start | bytes 38404
  219.3 41.6 %all-to-all-start.6 = ((bf16[4,64,3200]{2,1,0:T(8,128)(2,1)}), bf16[4,64,3200]{2,1,0:T(8,128)(2,1)S(1)}, u32[]{:S(2)}, u32[]{:S(2)}) async-start(bf16[4,64,3200]{2,1,0:T(8,128)(2,1)} %broadcast_in_dim.16), calls=%async_computation.6 | async-start | bytes 3276800 | tf_op jit(solution)/shard_map/all_to_all | solution.py:205
  261.1 6.6 %copy-start.3 = (bf16[5,4,160,640]{3,2,1,0:T(8,128)(2,1)S(1)}, bf16[5,4,160,640]{3,2,1,0:T(8,128)(2,1)}, u32[]{:S(2)}) copy-start(bf16[5,4,160,640]{3,2,1,0:T(8,128)(2,1)} %pad_maximum_fusion.3) | copy-start | bytes 12288004
  292.8 13.4 %all-to-all-start.9 = ((bf16[64,4,1280]{2,0,1:T(8,128)(2,1)}), bf16[64,4,1280]{2,0,1:T(8,128)(2,1)S(1)}, u32[]{:S(2)}, u32[]{:S(2)}) async-start(bf16[64,4,1280]{2,0,1:T(8,128)(2,1)} %copy.48), calls=%async_computation.9 | async-start | bytes 1310720 | tf_op jit(solution)/shard_map/all_to_all | solution.py:196
